TPU v7x, 32 devices: a whole 2x2x4 slice. The times are simulated.
32 devices in a mesh: grp: 2 (over core), mr: 8 (over z, y), mc: 2 (over x).
Axes of the slice: x: 2, y: 2, z: 4, core: 2. Of those that a mesh axis runs over, the one named last changes fastest.
Arguments:
- queries: bfloat16 [384, 8192], P(('grp', 'mr'), 'mc'), may hold values from -6 to 6
- new_keys: bfloat16 [384, 1024], P(('grp', 'mr'), 'mc'), may hold values from -6 to 6
- new_values: bfloat16 [384, 1024], P(('grp', 'mr'), 'mc'), may hold values from -6 to 6
- key_cache: bfloat16 [384, 512, 1024], P(('grp', 'mr'), None, 'mc'), may hold values from -6 to 6
- value_cache: bfloat16 [384, 512, 1024], P(('grp', 'mr'), None, 'mc'), may hold values from -6 to 6
- context_len: int32 [384], P(('grp', 'mr')), may hold values from 2 to 512, as said below
- cache_slot: int32 [384], P(('grp', 'mr')), may hold values from 0 to 383, as said below
- residual_in: bfloat16 [384, 8192], P(('grp', 'mr'), 'mc'), may hold values from -31 to 31
- out_weight: bfloat16 [8192, 8192], P(('grp', 'mr'), 'mc'), may hold values from -0.25 to 0.25
- gate_weight: bfloat16 [8192, 28672], P('mc', ('grp', 'mr')), may hold values from -0.0625 to 0.0625
- up_weight: bfloat16 [8192, 28672], P('mc', ('grp', 'mr')), may hold values from -0.0625 to 0.0625
Outputs:
- residual_out: bfloat16 [384, 8192], P(('grp', 'mr'), 'mc')
- activation: bfloat16 [384, 28672], P('mc', ('grp', 'mr'))
Inputs may be any that keep to these rules, and one draw needn't show every extreme that they name: Row r's history fills positions 0 to context_len[r] - 1 of its cache row; some row has 512. `cache_slot`: within each aligned block of 24 rows the values are a permutation of that block's own row indices.
All inputs are finite; a program needn't handle non-finite values.
Results may differ from a plain program's by a relative error of at most 0.006.
Values may be sent and summed in bfloat16 or wider, within the bound.
A program may use at most 128 MiB of HBM per device.

v0:
```python
import jax
import jax.numpy as jnp
from jax import lax
from jax.sharding import PartitionSpec as P

D = 8192
HD = 128


norm_epsilon = 1e-05
masked_score = -1e30


def attend_rows(queries, new_keys, new_values, key_rows, value_rows, context_len):
    row_denominator_sum = queries.shape[0]
    context = key_rows.shape[1]
    kv_heads = key_rows.shape[2] // HD
    groups = queries.shape[1] // key_rows.shape[2]
    attention_logit_scale = HD ** (-0.5)
    query_grouped_four = queries.reshape(row_denominator_sum, kv_heads, groups, HD)
    key_four = key_rows.reshape(row_denominator_sum, context, kv_heads, HD)
    value_four = value_rows.reshape(row_denominator_sum, context, kv_heads, HD)
    current_key = new_keys.reshape(row_denominator_sum, kv_heads, HD)
    own_value = new_values.reshape(row_denominator_sum, kv_heads, HD).astype(jnp.float32)
    scores = (
        jnp.einsum(
            "bkgd,bckd->bkgc", query_grouped_four, key_four, preferred_element_type=jnp.float32
        )
        * attention_logit_scale
    )
    positions = jnp.arange(context, dtype=jnp.int32)
    valid_mask = positions[None, :] < context_len[:, None]
    scores = jnp.where(valid_mask[:, None, None, :], scores, masked_score)
    current_score = (
        jnp.einsum(
            "cnhz,cnz->cnh", query_grouped_four, current_key, preferred_element_type=jnp.float32
        )
        * attention_logit_scale
    )
    row_max = jnp.maximum(jnp.max(scores, axis=3), current_score)
    exponent = jnp.exp(scores - row_max[..., None])
    own_exponent = jnp.exp(current_score - row_max)
    denominator = jnp.sum(exponent, axis=3) + own_exponent
    weights = (exponent / denominator[..., None]).astype(jnp.bfloat16)
    own_weight = (own_exponent / denominator).astype(jnp.bfloat16).astype(jnp.float32)
    combined = jnp.einsum(
        "bkgc,bckd->bkgd", weights, value_four, preferred_element_type=jnp.float32
    )
    combined = combined + own_weight[..., None] * own_value[:, :, None, :]
    return combined.reshape(row_denominator_sum, -1).astype(jnp.bfloat16)


def body(
    queries,
    new_keys,
    new_values,
    key_cache,
    value_cache,
    context_len,
    cache_slot,
    residual_in,
    out_weight,
    gate_weight,
    up_weight,
):
    local_rows = queries.shape[0]
    row_base = lax.axis_index(("grp", "mr")) * local_rows
    device_slot_index = cache_slot - row_base
    positions = jnp.arange(local_rows, dtype=jnp.int32)
    matches = device_slot_index[:, None] == positions[None, :]
    inverse = jnp.sum(jnp.where(matches, positions[:, None], 0), axis=0)
    by_cache = attend_rows(
        jnp.take(queries, inverse, axis=0),
        jnp.take(new_keys, inverse, axis=0),
        jnp.take(new_values, inverse, axis=0),
        key_cache,
        value_cache,
        jnp.take(context_len, inverse, axis=0),
    )
    attended = jnp.take(by_cache, device_slot_index, axis=0)
    gathered = lax.all_gather(attended, "mc", axis=1, tiled=True)
    features = lax.all_to_all(gathered, ("grp", "mr"), split_axis=1, concat_axis=0, tiled=True)
    groups = lax.axis_size("grp")
    rows = features.shape[0]
    group_rows = rows // groups
    group = lax.axis_index("grp")
    own_share = None
    for shift in range(groups - 1, -1, -1):
        target = lax.rem(group + shift, groups)
        block = lax.dynamic_slice_in_dim(features, target * group_rows, group_rows, axis=0)
        term = jnp.dot(block, out_weight, preferred_element_type=jnp.float32)
        if shift > 0:
            pairs = [(i, (i + shift) % groups) for i in range(groups)]
            term = lax.ppermute(term.astype(jnp.bfloat16), "grp", pairs).astype(jnp.float32)
        own_share = term if own_share is None else own_share + term
    shares = lax.psum_scatter(
        own_share.astype(jnp.bfloat16), "mr", scatter_dimension=0, tiled=True
    ).astype(jnp.float32)
    residual_out = (residual_in.astype(jnp.float32) + shares).astype(jnp.bfloat16)
    group_part = lax.all_gather(residual_out, "mr", axis=0, tiled=True)
    everyone = lax.all_gather(group_part, "grp", axis=0, tiled=True) if groups != 2 else None
    if groups == 2:
        other_part = lax.ppermute(group_part, "grp", [(0, 1), (1, 0)])
        first = jnp.where(group == 0, group_part, other_part)
        second = jnp.where(group == 0, other_part, group_part)
        everyone = jnp.concatenate([first, second], axis=0)
    widened = lax.optimization_barrier(everyone).astype(jnp.float32)
    squares = jnp.sum(widened * widened, axis=1)
    square_sum = scatter_sum(squares, jnp.float32)
    gate_term = jnp.dot(everyone, gate_weight, preferred_element_type=jnp.float32)
    gate_sum = scatter_sum(gate_term, jnp.bfloat16)
    up_term = jnp.dot(everyone, up_weight, preferred_element_type=jnp.float32)
    up_sum = scatter_sum(up_term, jnp.bfloat16)
    inverse_rms = lax.rsqrt(square_sum / D + norm_epsilon)
    gate_value = gate_sum * inverse_rms[:, None]
    upward = up_sum * inverse_rms[:, None]
    activation = (jax.nn.silu(gate_value) * upward).astype(jnp.bfloat16)
    return (residual_out, activation)


def scatter_sum(term, kind):
    count = lax.axis_size("mc")
    me = lax.axis_index("mc")
    kept = term.shape[0] // count
    total = lax.dynamic_slice_in_dim(term, me * kept, kept, axis=0)
    for shift in range(1, count):
        target = lax.rem(me + shift, count)
        sent = lax.dynamic_slice_in_dim(term, target * kept, kept, axis=0).astype(kind)
        pairs = [(i, (i + shift) % count) for i in range(count)]
        total = total + lax.ppermute(sent, "mc", pairs).astype(jnp.float32)
    return total


def solution(mesh):
    in_specs = (
        P(("grp", "mr"), "mc"),
        P(("grp", "mr"), "mc"),
        P(("grp", "mr"), "mc"),
        P(("grp", "mr"), None, "mc"),
        P(("grp", "mr"), None, "mc"),
        P(("grp", "mr")),
        P(("grp", "mr")),
        P(("grp", "mr"), "mc"),
        P(("grp", "mr"), "mc"),
        P("mc", ("grp", "mr")),
        P("mc", ("grp", "mr")),
    )
    out_specs = (P(("grp", "mr"), "mc"), P("mc", ("grp", "mr")))
    return jax.shard_map(body, mesh=mesh, in_specs=in_specs, out_specs=out_specs, check_vma=False)
```

profile of v0, /device:TPU:0, one launch (start us, length us, event | category | flops | bytes accessed | tf_op | source)
XLA Modules:
  0.0 235.8 jit_solution(16639397591601032340)
XLA Ops:
  7.2 0.0 copy-start
  7.2 0.7 compare_and_fusion
  7.9 0.1 select_reduce_fusion
  8.0 1.4 gather_fusion
  9.4 1.4 gather_fusion.2
  10.7 1.4 gather_fusion.3
  12.1 0.1 select_convert_fusion
  12.2 0.0 copy-done
  12.2 0.7 gather_fusion.1
  12.9 0.1 select_bitcast_fusion
  13.0 0.1 iota_compare_fusion
  13.1 0.2 fusion.30
  13.3 6.5 %fusion.29 = (f32[24,4,8]{2,1,0:T(4,128)S(1)}, f32[24,4,8,512]{3,2,1,0:T(8,128)S(1)}) fusion(bf16[24,4,8,128]{3,2,1,0:T(8,128)(2,1)S(1)} %bitcast.56, pred[24,512]{1,0:T(8,128)(4,1)S(1)} %iota_compare_fusion, bf16[24,512,512]{2,1,0:T(8,128)(2,1)} %param.18), kind=kOutput, calls=%fused_computation.62 | convolution fusion | flops 101842176 | bytes 14367744 | tf_op jit(solution)/shard_map/bkgd,bckd->bkgc/dot_general | solution.py:26
  19.8 0.5 fusion.8
  20.4 5.8 %fusion.12 = bf16[24,4,8,128]{3,2,1,0:T(8,128)(2,1)S(1)} fusion(f32[24,4,8,512]{3,2,1,0:T(8,128)S(1)} %get-tuple-element.16, f32[24,4,8]{2,1,0:T(4,128)S(1)} %get-tuple-element.11, f32[24,4,8]{2,1,0:T(4,128)S(1)} %multiply_maximum_fusion, f32[24,4,128]{2,1,0:T(4,128)S(1)} %reshape.91, f32[24,4,8]{2,1,0:T(4,128)S(1)} %get-tuple-element.10, ...), kind=kOutput, calls=%fused_computation.25 | convolution fusion | flops 102137856 | bytes 14410752 | tf_op jit(solution)/shard_map/bkgc,bckd->bkgd/dot_general | solution.py:46
  26.2 0.1 copy.47
  26.3 0.7 gather_fusion.4
  27.0 0.1 broadcast_select_fusion.2
  27.1 8.5 %all_gather.6 = bf16[24,8192]{1,0:T(8,128)(2,1)S(1)} all-gather(bf16[24,4096]{1,0:T(8,128)(2,1)S(1)} %broadcast_select_fusion.2), channel_id=1, replica_groups=mesh['grp'=2,'mr'=8,'mc'=2] {'mc'}, dimensions={1}, use_global_device_ids=true | all-gather | bytes 589824 | tf_op jit(solution)/shard_map/all_gather | solution.py:81
  35.6 0.8 copy.46
  36.4 6.2 %all-to-all-start = ((bf16[24,16,512]{2,0,1:T(8,128)(2,1)}), bf16[24,16,512]{2,0,1:T(8,128)(2,1)S(1)}, u32[]{:S(2)}, u32[]{:S(2)}) async-start(bf16[24,16,512]{2,0,1:T(8,128)(2,1)} %bitcast.49), calls=%async_computation | async-start | bytes 786432 | tf_op jit(solution)/shard_map/all_to_all | solution.py:82
  42.5 0.0 reduce-scatter.2.cloned.1.call-start
  42.6 13.0 %all-to-all-done = bf16[24,16,512]{2,0,1:T(8,128)(2,1)S(1)} async-done(((bf16[24,16,512]{2,0,1:T(8,128)(2,1)}), bf16[24,16,512]{2,0,1:T(8,128)(2,1)S(1)}, u32[]{:S(2)}, u32[]{:S(2)}) %all-to-all-start) | async-done | bytes 393248 | tf_op jit(solution)/shard_map/all_to_all | solution.py:82
  55.6 4.4 %convolution_convert_fusion = bf16[192,4096]{1,0:T(8,128)(2,1)} fusion(bf16[512,4096]{1,0:T(8,128)(2,1)} %param.23, bf16[384,512]{1,0:T(8,128)(2,1)S(1)} %bitcast.52, s32[]{:T(128)S(6)} %select_n.80), kind=kOutput, calls=%fused_computation.12 | convolution fusion | flops 806092800 | bytes 5963780 | tf_op jit(solution)/shard_map/dot_general | solution.py:91
  60.0 0.0 collective-permute-start
  60.0 3.6 %collective-permute-done = bf16[192,4096]{1,0:T(8,128)(2,1)S(1)} collective-permute-done((bf16[192,4096]{1,0:T(8,128)(2,1)}, bf16[192,4096]{1,0:T(8,128)(2,1)S(1)}, u32[]{:S(2)}, u32[]{:S(2)}) %collective-permute-start) | collective-permute-done | bytes 1572896 | tf_op jit(solution)/shard_map/ppermute | solution.py:94
  63.6 4.4 %add_convert_fusion = bf16[192,4096]{1,0:T(8,128)(2,1)} fusion(bf16[192,4096]{1,0:T(8,128)(2,1)S(1)} %collective-permute-done, bf16[512,4096]{1,0:T(8,128)(2,1)} %param.23, bf16[384,512]{1,0:T(8,128)(2,1)S(1)} %bitcast.53, s32[]{:T(128)S(6)} %select_n.81), kind=kOutput, calls=%fused_computation.14 | convolution fusion | flops 807665664 | bytes 7536644 | tf_op jit(solution)/shard_map/dot_general | solution.py:91
  67.9 0.0 reduce-scatter.2.cloned.1.call-update
  68.0 0.2 all-gather.2.cloned.1.call-start
  68.2 63.5 %reduce-scatter.2.cloned.1.call-done = bf16[24,4096]{1,0:T(8,128)(2,1)} async-done(((bf16[192,4096]{1,0:T(8,128)(2,1)}), bf16[24,4096]{1,0:T(8,128)(2,1)}) %reduce-scatter.2.cloned.1.call-update) | async-done | bytes 196624 | tf_op jit(solution)/shard_map/reduce_scatter | solution.py:96
  131.7 0.0 copy-done.3
  131.7 1.6 add_convert_fusion.1
  133.3 0.0 all-gather.2.cloned.1.call-update
  133.4 44.1 %all-gather.2.cloned.1.call-done = bf16[192,4096]{1,0:T(8,128)(2,1)} async-done(((bf16[24,4096]{1,0:T(8,128)(2,1)}), bf16[192,4096]{1,0:T(8,128)(2,1)}) %all-gather.2.cloned.1.call-update) | async-done | bytes 1572880 | tf_op jit(solution)/shard_map/all_gather | solution.py:100
  177.5 0.0 collective-permute-start.1
  177.5 3.6 %collective-permute-done.1 = bf16[192,4096]{1,0:T(8,128)(2,1)S(1)} collective-permute-done((bf16[192,4096]{1,0:T(8,128)(2,1)}, bf16[192,4096]{1,0:T(8,128)(2,1)S(1)}, u32[]{:S(2)}, u32[]{:S(2)}) %collective-permute-start.1) | collective-permute-done | bytes 1572896 | tf_op jit(solution)/shard_map/ppermute | solution.py:103
  181.1 0.0 slice-start
  181.1 1.8 broadcast_select_fusion.1
  182.9 0.0 slice-start.1
  182.9 0.0 slice-start.2
  182.9 0.0 slice-start.3
  182.9 9.3 %fusion.28 = f32[384,1792]{1,0:T(8,128)S(1)} fusion(bf16[4096,1792]{1,0:T(8,128)(2,1)} %param.24, bf16[192,4096]{1,0:T(8,128)(2,1)S(1)} %get-tuple-element.9, bf16[192,4096]{1,0:T(8,128)(2,1)S(1)} %get-tuple-element.8), kind=kOutput, calls=%fused_computation.61 | convolution fusion | flops 5643436032 | bytes 20578304 | tf_op jit(solution)/shard_map/dot_general | solution.py:110
  192.2 0.9 dynamic-slice_convert_fusion.1
  193.2 1.5 collective-permute-start.2
  194.6 0.0 slice-done
  194.6 0.0 slice-done.1
  194.6 0.0 slice-done.2
  194.6 0.0 slice-done.3
  194.7 5.9 %fusion.27 = f32[384,1792]{1,0:T(8,128)S(1)} fusion(bf16[4096,1792]{1,0:T(8,128)(2,1)S(1)} %bitcast.61, bf16[192,4096]{1,0:T(8,128)(2,1)S(1)} %get-tuple-element.9, bf16[192,4096]{1,0:T(8,128)(2,1)S(1)} %get-tuple-element.8), kind=kOutput, calls=%fused_computation.60 | convolution fusion | flops 5643436032 | bytes 20578304 | tf_op jit(solution)/shard_map/dot_general | solution.py:112
  200.5 0.0 copy-start.2
  200.5 1.0 dynamic-slice_convert_fusion
  201.5 0.6 collective-permute-start.4
  202.1 0.2 pad_maximum_fusion
  202.3 0.0 copy-done.2
  202.3 0.0 copy-start.1
  202.3 0.7 multiply_reduce_fusion
  203.0 0.1 dynamic_slice.29
  203.1 1.5 collective-permute-start.3
  204.6 21.1 %collective-permute-done.3 = f32[192]{0:T(256)S(1)} collective-permute-done((f32[192]{0:T(256)S(1)}, f32[192]{0:T(256)S(1)}, u32[]{:S(2)}, u32[]{:S(2)}) %collective-permute-start.3) | collective-permute-done | bytes 800 | tf_op jit(solution)/shard_map/ppermute | solution.py:130
  225.7 0.1 add_rsqrt_fusion
  225.8 0.0 collective-permute-done.2
  225.8 0.0 collective-permute-done.4
  225.8 3.2 %multiply_convert_fusion = bf16[192,1792]{1,0:T(8,128)(2,1)} fusion(bf16[192,1792]{1,0:T(8,128)(2,1)} %collective-permute-done.4, f32[384,1792]{1,0:T(8,128)} %copy-done.2, s32[]{:T(128)S(6)} %select_n.85, bf16[192,1792]{1,0:T(8,128)(2,1)} %collective-permute-done.2, f32[384,1792]{1,0:T(8,128)S(1)} %fusion.28, f32[192]{0:T(256)S(1)} %add_rsqrt_fusion), kind=kLoop, calls=%fused_computation.21 | loop fusion | flops 4128768 | bytes 4817668 | tf_op jit(solution)/shard_map/convert_element_type | solution.py:117
  229.0 0.0 copy-done.1
  (12 shorter events, 0.2 us)
Async XLA Ops:
  7.2 5.0 %copy-start = (bf16[24,4096]{1,0:T(8,128)(2,1)S(1)}, bf16[24,4096]{1,0:T(8,128)(2,1)}, u32[]{:S(2)}) copy-start(bf16[24,4096]{1,0:T(8,128)(2,1)} %param.15) | copy-start | bytes 589828
  36.4 19.3 %all-to-all-start = ((bf16[24,16,512]{2,0,1:T(8,128)(2,1)}), bf16[24,16,512]{2,0,1:T(8,128)(2,1)S(1)}, u32[]{:S(2)}, u32[]{:S(2)}) async-start(bf16[24,16,512]{2,0,1:T(8,128)(2,1)} %bitcast.49), calls=%async_computation | async-start | bytes 786432 | tf_op jit(solution)/shard_map/all_to_all | solution.py:82
  42.5 89.1 %reduce-scatter.2.cloned.1.call-start = ((), (), s32[]{:S(2)}) async-start(), calls=%async_computation.2 | async-start | bytes 1769472 | tf_op jit(solution)/shard_map/reduce_scatter | solution.py:96
  60.0 3.6 %collective-permute-start = (bf16[192,4096]{1,0:T(8,128)(2,1)}, bf16[192,4096]{1,0:T(8,128)(2,1)S(1)}, u32[]{:S(2)}, u32[]{:S(2)}) collective-permute-start(bf16[192,4096]{1,0:T(8,128)(2,1)} %convolution_convert_fusion), channel_id=1, source_target_pairs={{0,16},{16,0},{1,17},{17,1},{2,18},{18,2},{3,19},{19,3},{4,20},{20... | collective-permute-start | bytes 4718600 | tf_op jit(solution)/shard_map/ppermute | solution.py:94
  60.0 71.7 %copy-start.3 = (bf16[24,4096]{1,0:T(8,128)(2,1)S(1)}, bf16[24,4096]{1,0:T(8,128)(2,1)}, u32[]{:S(2)}) copy-start(bf16[24,4096]{1,0:T(8,128)(2,1)} %param.22) | copy-start | bytes 589828
  68.0 109.5 %all-gather.2.cloned.1.call-start = ((), (), s32[]{:S(2)}) async-start(), calls=%async_computation.3 | async-start | bytes 1769472 | tf_op jit(solution)/shard_map/all_gather | solution.py:100
  177.5 3.6 %collective-permute-start.1 = (bf16[192,4096]{1,0:T(8,128)(2,1)}, bf16[192,4096]{1,0:T(8,128)(2,1)S(1)}, u32[]{:S(2)}, u32[]{:S(2)}) collective-permute-start(bf16[192,4096]{1,0:T(8,128)(2,1)} %all-gather.2.cloned.1.call-done), channel_id=1, source_target_pairs={{0,16},{16,0},{1,17},{17,1},{2,18},{18,2},{3,19},{19,3},{4,20},{20... | collective-permute-start | bytes 4718600 | tf_op jit(solution)/shard_map/ppermute | solution.py:103
  181.1 13.5 %slice-start = ((s8[14680064]{0:T(1024)(128)(4,1)}), s8[4194304]{0:T(1024)(128)(4,1)S(1)}, s32[]{:S(2)}) async-start(s8[14680064]{0:T(1024)(128)(4,1)} %bitcast.60), calls=%async_computation.4 | async-start | bytes 8388608
  182.9 11.7 %slice-start.1 = ((s8[14680064]{0:T(1024)(128)(4,1)}), s8[4194304]{0:T(1024)(128)(4,1)S(1)}, s32[]{:S(2)}) async-start(s8[14680064]{0:T(1024)(128)(4,1)} %bitcast.60), calls=%async_computation.5 | async-start | bytes 8388608
  182.9 11.7 %slice-start.2 = ((s8[14680064]{0:T(1024)(128)(4,1)}), s8[4194304]{0:T(1024)(128)(4,1)S(1)}, s32[]{:S(2)}) async-start(s8[14680064]{0:T(1024)(128)(4,1)} %bitcast.60), calls=%async_computation.6 | async-start | bytes 8388608
  182.9 11.7 %slice-start.3 = ((s8[14680064]{0:T(1024)(128)(4,1)}), s8[2097152]{0:T(1024)(128)(4,1)S(1)}, s32[]{:S(2)}) async-start(s8[14680064]{0:T(1024)(128)(4,1)} %bitcast.60), calls=%async_computation.7 | async-start | bytes 4194304
  193.2 32.6 %collective-permute-start.2 = (bf16[192,1792]{1,0:T(8,128)(2,1)}, bf16[192,1792]{1,0:T(8,128)(2,1)}, u32[]{:S(2)}, u32[]{:S(2)}) collective-permute-start(bf16[192,1792]{1,0:T(8,128)(2,1)} %dynamic-slice_convert_fusion.1), channel_id=1, source_target_pairs={{0,1},{1,0},{2,3},{3,2},{4,5},{5,4},{6,7},{7,6},{8,9},{9,8},{10,11... | collective-permute-start | bytes 2064392 | tf_op jit(solution)/shard_map/ppermute | solution.py:130
  200.5 1.8 copy-start.2
  201.5 24.3 %collective-permute-start.4 = (bf16[192,1792]{1,0:T(8,128)(2,1)}, bf16[192,1792]{1,0:T(8,128)(2,1)}, u32[]{:S(2)}, u32[]{:S(2)}) collective-permute-start(bf16[192,1792]{1,0:T(8,128)(2,1)} %dynamic-slice_convert_fusion), channel_id=1, source_target_pairs={{0,1},{1,0},{2,3},{3,2},{4,5},{5,4},{6,7},{7,6},{8,9},{9,8},{10,11... | collective-permute-start | bytes 2064392 | tf_op jit(solution)/shard_map/ppermute | solution.py:130
  202.3 26.7 %copy-start.1 = (bf16[24,4096]{1,0:T(8,128)(2,1)S(1)}, bf16[24,4096]{1,0:T(8,128)(2,1)}, u32[]{:S(2)}) copy-start(bf16[24,4096]{1,0:T(8,128)(2,1)} %param.15) | copy-start | bytes 589828
  203.1 22.6 %collective-permute-start.3 = (f32[192]{0:T(256)S(1)}, f32[192]{0:T(256)S(1)}, u32[]{:S(2)}, u32[]{:S(2)}) collective-permute-start(f32[192]{0:T(256)S(1)} %dynamic_slice.29), channel_id=1, source_target_pairs={{0,1},{1,0},{2,3},{3,2},{4,5},{5,4},{6,7},{7,6},{8,9},{9,8},{10,11... | collective-permute-start | bytes 2312 | tf_op jit(solution)/shard_map/ppermute | solution.py:130
Sparse Core Ops, SparseCore 0:
  68.1 63.5 reduce-scatter.1
  134.5 43.0 all-gather.1
where the time goes:
time: 236 us
  waiting for transfers between devices  149 us (63%)
  matrix products  36.3 us (15%)
  between operations  14.3 us (6%)
  starting transfers between devices  9.95 us (4%)
  other arithmetic  9.32 us (4%)
  blocking collectives  8.53 us (4%)
  local copies, waits for them, and re-layouts  8.38 us (4%)
    reduce_scatter x1, waiting for transfers between devices, body(): lax.psum_scatter(own_share.astype(jnp.bfloat16), 'mr', scatter_dimension=...  63.5 us
    all_gather x1, waiting for transfers between devices, body(): group_part = lax.all_gather(residual_out, 'mr', axis=0, tiled=True)  44.1 us
    ppermute x3, waiting for transfers between devices, scatter_sum(): total = total + lax.ppermute(sent, 'mc', pairs).astype(jnp.float32)  21.1 us
    all_to_all x1, waiting for transfers between devices, body(): lax.all_to_all(gathered, ('grp', 'mr'), split_axis=1, concat_axis=0, tile...  13 us
    dot_general x1, matrix products, body(): jnp.dot(everyone, gate_weight, preferred_element_type=jnp.float32)  9.31 us
    dot_general x2, matrix products, body(): term = jnp.dot(block, out_weight, preferred_element_type=jnp.float32)  8.72 us
    all_gather x1, blocking collectives, body(): gathered = lax.all_gather(attended, 'mc', axis=1, tiled=True)  8.53 us
    dot_general x1, matrix products, attend_rows(): jnp.einsum('bkgd,bckd->bkgc', query_grouped_four, key_four, preferred_ele...  6.45 us
  transfers between devices with their start and end apart: 8, of which 6 were waited for; matrix products, arithmetic and copies ran while one was open for 3% of the time, Pallas kernels for 0%

commit v1 on v0

v1 whole, which is shorter than its diff:
```python
import functools

import jax
import jax.numpy as jnp
from jax import lax
from jax.experimental import pallas as pl
from jax.experimental.pallas import tpu as pltpu
from jax.sharding import PartitionSpec as P

D = 8192
HD = 128


norm_epsilon = 1e-05
masked_score = -1e30


def attend_rows(queries, new_keys, new_values, key_rows, value_rows, context_len):
    row_denominator_sum = queries.shape[0]
    context = key_rows.shape[1]
    kv_heads = key_rows.shape[2] // HD
    groups = queries.shape[1] // key_rows.shape[2]
    attention_logit_scale = HD ** (-0.5)
    query_grouped_four = queries.reshape(row_denominator_sum, kv_heads, groups, HD)
    key_four = key_rows.reshape(row_denominator_sum, context, kv_heads, HD)
    value_four = value_rows.reshape(row_denominator_sum, context, kv_heads, HD)
    current_key = new_keys.reshape(row_denominator_sum, kv_heads, HD)
    own_value = new_values.reshape(row_denominator_sum, kv_heads, HD).astype(jnp.float32)
    scores = (
        jnp.einsum(
            "bkgd,bckd->bkgc", query_grouped_four, key_four, preferred_element_type=jnp.float32
        )
        * attention_logit_scale
    )
    positions = jnp.arange(context, dtype=jnp.int32)
    valid_mask = positions[None, :] < context_len[:, None]
    scores = jnp.where(valid_mask[:, None, None, :], scores, masked_score)
    current_score = (
        jnp.einsum(
            "cnhz,cnz->cnh", query_grouped_four, current_key, preferred_element_type=jnp.float32
        )
        * attention_logit_scale
    )
    row_max = jnp.maximum(jnp.max(scores, axis=3), current_score)
    exponent = jnp.exp(scores - row_max[..., None])
    own_exponent = jnp.exp(current_score - row_max)
    denominator = jnp.sum(exponent, axis=3) + own_exponent
    weights = (exponent / denominator[..., None]).astype(jnp.bfloat16)
    own_weight = (own_exponent / denominator).astype(jnp.bfloat16).astype(jnp.float32)
    combined = jnp.einsum(
        "bkgc,bckd->bkgd", weights, value_four, preferred_element_type=jnp.float32
    )
    combined = combined + own_weight[..., None] * own_value[:, :, None, :]
    return combined.reshape(row_denominator_sum, -1).astype(jnp.bfloat16)


MESH = pl.DeviceIdType.MESH
SUBS = 4


def remote(src, dst, send_sem, recv_sem, device):
    return pltpu.make_async_remote_copy(
        src_ref=src,
        dst_ref=dst,
        send_sem=send_sem,
        recv_sem=recv_sem,
        device_id=device,
        device_id_type=MESH,
    )


def layer_kernel(
    sizes,
    att,
    res_in,
    w_hbm,
    gate_hbm,
    up_hbm,
    res_out,
    act_out,
    w_buf,
    gate_buf,
    up_buf,
    res_peer,
    disp,
    feats,
    acc,
    rs_send,
    rs_recv,
    xg,
    squares,
    sq_send,
    sq_recv,
    result,
    keep,
    ex_send,
    ex_recv,
    load_sem,
    peer_send_sem,
    peer_recv_sem,
    disp_send_sem,
    disp_recv_sem,
    fwd_send_sem,
    fwd_recv_sem,
    rs_send_sem,
    rs_recv_sem,
    ag_send_sem,
    ag_recv_sem,
    half_send_sem,
    half_recv_sem,
    sq_send_sem,
    sq_recv_sem,
    ex_send_sem,
    ex_recv_sem,
):
    groups, n, parts = sizes
    h = n // 2
    g = lax.axis_index("grp")
    m = lax.axis_index("mr")
    c = lax.axis_index("mc")
    peer = (1 - g, m, c)
    rows, width = att.shape
    feat = w_hbm.shape[0]
    half = width // 2
    sub = half // SUBS
    blocks = width // feat
    tile = result.shape[3]
    tiles = act_out.shape[1] // tile
    kept = act_out.shape[0]

    def chip_at(q):
        q = lax.rem(q + 2 * n, n)
        t = q // h
        return (1 - t) * 2 * q + t * (2 * n - 1 - 2 * q)

    place = (1 - m % 2) * (m // 2) + (m % 2) * (n - 1 - m // 2)
    right = (g, chip_at(place + 1), c)
    left = (g, chip_at(place - 1), c)

    w_load = pltpu.make_async_copy(
        w_hbm.at[:, pl.ds(pl.multiple_of(g * half, half), half)], w_buf.at[g], load_sem.at[0]
    )
    gate_load = pltpu.make_async_copy(gate_hbm, gate_buf, load_sem.at[1])
    up_load = pltpu.make_async_copy(up_hbm, up_buf, load_sem.at[2])
    w_load.start()

    barrier = pltpu.get_barrier_semaphore()
    total = groups * n * parts
    me = (g * n + m) * parts + c

    def greet(i, carry):
        other = lax.rem(me + i, total)
        device = (other // (n * parts), (other // parts) % n, other % parts)
        pl.semaphore_signal(barrier, inc=1, device_id=device, device_id_type=MESH)
        return carry

    lax.fori_loop(1, total, greet, 0)
    pl.semaphore_wait(barrier, total - 1)

    pending = []
    own_slot = g * n + m

    for k in range(parts):
        for j in range(blocks):
            jj = lax.rem(m + j, blocks)
            block = c * blocks + jj
            device = (block // n, block % n, lax.rem(c + k, parts))
            copy = remote(
                att.at[:, pl.ds(pl.multiple_of(jj * feat, feat), feat)],
                disp.at[block // n, own_slot],
                disp_send_sem.at[k, j],
                disp_recv_sem.at[own_slot],
                device,
            )
            if k == 0:
                pl.when(block != own_slot)(copy.start)

                @pl.when(block == own_slot)
                def _():
                    disp[g, own_slot] = att[:, pl.ds(pl.multiple_of(jj * feat, feat), feat)]

                pending.append((copy, block != own_slot))
            else:
                copy.start()
                pending.append((copy, None))

    other_cols = pl.ds(pl.multiple_of((1 - g) * half, half), half)
    own_cols = pl.ds(pl.multiple_of(g * half, half), half)
    w_share = remote(
        w_hbm.at[:, other_cols], w_buf.at[g], peer_send_sem.at[0], peer_recv_sem.at[0], peer
    )
    w_share.start()
    res_share = remote(
        res_in.at[:, other_cols], res_peer, peer_send_sem.at[1], peer_recv_sem.at[1], peer
    )
    res_share.start()
    pending += [(w_share, None), (res_share, None)]
    gate_load.start()
    up_load.start()

    source = own_slot // blocks
    from_self = c == source
    for i in range(groups * n):
        arrived = remote(
            disp.at[g, i], disp.at[g, i], disp_send_sem.at[0, 0], disp_recv_sem.at[i], peer
        )
        is_remote = jnp.logical_or(source != c, own_slot != i)
        pl.when(is_remote)(arrived.wait_recv)
        forward = remote(
            disp.at[g, i], disp.at[g, i], fwd_send_sem.at[i], fwd_recv_sem.at[i], peer
        )
        forward.start()
        pending.append((forward, None))
    for i in range(groups * n):
        remote(
            disp.at[1 - g, i], disp.at[1 - g, i], fwd_send_sem.at[i], fwd_recv_sem.at[i], peer
        ).wait_recv()
    for i in range(n):
        for k in range(groups):
            pair = [disp[k, gg * n + i].astype(jnp.float32) for gg in range(groups)]
            feats[i, :, k * feat : (k + 1) * feat] = jnp.concatenate(pair, axis=0).astype(
                jnp.bfloat16
            )
    w_load.wait()
    w_share.wait_recv()
    res_share.wait_recv()

    step_cols = min(512, half)

    def project(t, carry):
        cols = pl.ds(pl.multiple_of(t * step_cols, step_cols), step_cols)
        value = jnp.dot(
            feats[...].reshape(n * groups * rows, groups * feat),
            w_buf[:, :, cols].reshape(groups * feat, step_cols),
            preferred_element_type=jnp.float32,
        )
        acc[:, :, cols] = value.reshape(n, groups * rows, step_cols)
        return carry

    lax.fori_loop(0, half // step_cols, project, 0)

    def travels(direction, k):
        return (k < SUBS // 2) == (direction == 0)

    def rs_copy(direction, s, k):
        cols = pl.ds(k * sub, sub)
        return remote(
            rs_send.at[direction, s, :, cols],
            rs_recv.at[direction, s, :, cols],
            rs_send_sem.at[direction, s, k],
            rs_recv_sem.at[direction, s, k],
            right if direction == 0 else left,
        )

    for s in range(h):
        for k in range(SUBS):
            for direction in range(2):
                if s == 0 and not travels(direction, k):
                    continue
                cols = pl.ds(k * sub, sub)
                goal = chip_at(place + h - s if direction == 0 else place - h + s)
                value = acc[goal, :, cols]
                if s > 1 or (s == 1 and travels(direction, k)):
                    rs_copy(direction, s - 1, k).wait_recv()
                    value = value + rs_recv[direction, s - 1, :, cols].astype(jnp.float32)
                rs_send[direction, s, :, cols] = value.astype(jnp.bfloat16)
                copy = rs_copy(direction, s, k)
                copy.start()
                pending.append((copy, None))

    def ag_copy(direction, s, k, holder):
        cols = pl.ds(pl.multiple_of(g * half + k * sub, sub), sub)
        return remote(
            xg.at[holder, :, cols],
            xg.at[holder, :, cols],
            ag_send_sem.at[direction, s, k],
            ag_recv_sem.at[direction, s, k],
            right if direction == 0 else left,
        )

    def half_copy(holder, side, slot, k):
        cols = pl.ds(pl.multiple_of(side * half + k * sub, sub), sub)
        return remote(
            xg.at[holder, :, cols],
            xg.at[holder, :, cols],
            half_send_sem.at[slot, k],
            half_recv_sem.at[slot, k],
            peer,
        )

    def add_squares(holder):
        wide = xg[holder].astype(jnp.float32)
        summed = jnp.sum(wide * wide, axis=1, keepdims=True)
        squares[holder] = jnp.broadcast_to(summed, (groups * rows, 128)).reshape(groups, rows, 128)

    for k in range(SUBS):
        cols = pl.ds(k * sub, sub)
        for direction in range(2):
            rs_copy(direction, h - 1, k).wait_recv()
        mine = res_in[:, pl.ds(pl.multiple_of(g * half + k * sub, sub), sub)].astype(jnp.float32)
        other = res_peer[:, cols].astype(jnp.float32)
        first = jnp.where(g == 0, mine, other)
        second = jnp.where(g == 0, other, mine)
        value = acc[m, :, cols]
        for direction in range(2):
            value = value + rs_recv[direction, h - 1, :, cols].astype(jnp.float32)
        value = value + jnp.concatenate([first, second], axis=0)
        xg[m, :, pl.ds(pl.multiple_of(g * half + k * sub, sub), sub)] = value.astype(jnp.bfloat16)
        for direction in range(2):
            if h > 1 or travels(direction, k):
                copy = ag_copy(direction, 0, k, m)
                copy.start()
                pending.append((copy, None))
        copy = half_copy(m, g, 0, k)
        copy.start()
        pending.append((copy, None))

    def finish(slots):
        for holder, slot in slots:
            for k in range(SUBS):
                half_copy(holder, 1 - g, slot, k).wait_recv()
            add_squares(holder)

    waiting = [(m, 0)]
    for s in range(h):
        arrivals = []
        for k in range(SUBS):
            for direction in range(2):
                last = s == h - 1
                if last and not travels(direction, k):
                    continue
                holder = chip_at(place - 1 - s if direction == 0 else place + 1 + s)
                slot = n - 1 if last else 1 + 2 * s + direction
                ag_copy(direction, s, k, holder).wait_recv()
                if s + 1 < h and (s + 1 < h - 1 or travels(direction, k)):
                    copy = ag_copy(direction, s + 1, k, holder)
                    copy.start()
                    pending.append((copy, None))
                copy = half_copy(holder, g, slot, k)
                copy.start()
                pending.append((copy, None))
                if k == 0 or (last and k == SUBS // 2):
                    if not (last and arrivals):
                        arrivals.append((holder, slot))
        finish(waiting)
        waiting = arrivals
    finish(waiting)

    both = xg[m].astype(jnp.float32)
    res_out[...] = jnp.where(g == 0, both[:rows], both[rows:]).astype(jnp.bfloat16)

    per_group = parts // groups
    count = n // per_group

    def span(target):
        return pl.ds((target % per_group) * count, count), target // per_group

    def sq_copy(k):
        return remote(
            sq_send.at[k - 1],
            sq_recv.at[k - 1],
            sq_send_sem.at[k - 1],
            sq_recv_sem.at[k - 1],
            (g, m, lax.rem(c + k, parts)),
        )

    for k in range(1, parts):
        chips, group = span(lax.rem(c + k, parts))
        sq_send[k - 1] = squares[chips, group]
        copy = sq_copy(k)
        copy.start()
        pending.append((copy, None))

    gate_load.wait()
    up_load.wait()

    def ex_copy(k, w, t):
        return remote(
            ex_send.at[k - 1, w, t],
            ex_recv.at[k - 1, w, t],
            ex_send_sem.at[k - 1, w, t],
            ex_recv_sem.at[k - 1, w, t],
            (g, m, lax.rem(c + k, parts)),
        )

    def expand(t, carry):
        cols = pl.ds(pl.multiple_of(t * tile, tile), tile)
        for w, weights in enumerate((gate_buf, up_buf)):
            value = jnp.dot(
                xg[...].reshape(n * groups * rows, width),
                weights[:, cols],
                preferred_element_type=jnp.float32,
            )
            result[...] = value.reshape(n, groups, rows, tile)
            for k in range(1, parts):
                chips, group = span(lax.rem(c + k, parts))
                ex_send[k - 1, w, t] = (
                    result[chips, group].reshape(kept, tile).astype(jnp.bfloat16)
                )
                ex_copy(k, w, t).start()
            chips, group = span(c)
            keep[w, t] = result[chips, group].reshape(kept, tile)
        return carry

    lax.fori_loop(0, tiles, expand, 0)

    chips, group = span(c)
    summed = squares[chips, group]
    for k in range(1, parts):
        sq_copy(k).wait_recv()
        summed = summed + sq_recv[k - 1]
    inverse = lax.rsqrt(summed / D + norm_epsilon).reshape(kept, 128)[:, :1]

    def activate(t, carry):
        sums = []
        for w in range(2):
            value = keep[w, t]
            for k in range(1, parts):
                ex_copy(k, w, t).wait()
                value = value + ex_recv[k - 1, w, t].astype(jnp.float32)
            sums.append(value * inverse)
        gate, up = sums
        cols = pl.ds(pl.multiple_of(t * tile, tile), tile)
        act_out[:, cols] = (gate / (1.0 + jnp.exp(-gate)) * up).astype(jnp.bfloat16)
        return carry

    lax.fori_loop(0, tiles, activate, 0)

    for copy, condition in pending:
        if condition is None:
            copy.wait_send()
        else:
            pl.when(condition)(copy.wait_send)


def layer(sizes, attended, residual_in, out_weight, gate_weight, up_weight):
    groups, n, parts = sizes
    h = n // 2
    rows, width = attended.shape
    feat = out_weight.shape[0]
    half = width // 2
    hidden = gate_weight.shape[1]
    tile = 256 if hidden % 256 == 0 else 128
    tiles = hidden // tile
    kept = groups * n * rows // parts
    bf16, f32 = jnp.bfloat16, jnp.float32
    dma = pltpu.SemaphoreType.DMA
    vmem = pl.BlockSpec(memory_space=pltpu.VMEM)
    anywhere = pl.BlockSpec(memory_space=pl.ANY)
    blocks = width // feat
    return pl.pallas_call(
        functools.partial(layer_kernel, sizes),
        out_shape=(
            jax.ShapeDtypeStruct((rows, width), bf16),
            jax.ShapeDtypeStruct((kept, hidden), bf16),
        ),
        in_specs=[vmem, vmem, anywhere, anywhere, anywhere],
        out_specs=(vmem, vmem),
        scratch_shapes=[
            pltpu.VMEM((groups, feat, half), bf16),
            pltpu.VMEM(gate_weight.shape, bf16),
            pltpu.VMEM(up_weight.shape, bf16),
            pltpu.VMEM((rows, half), bf16),
            pltpu.VMEM((groups, groups * n, rows, feat), bf16),
            pltpu.VMEM((n, groups * rows, groups * feat), bf16),
            pltpu.VMEM((n, groups * rows, half), f32),
            pltpu.VMEM((2, h, groups * rows, half), bf16),
            pltpu.VMEM((2, h, groups * rows, half), bf16),
            pltpu.VMEM((n, groups * rows, width), bf16),
            pltpu.VMEM((n, groups, rows, 128), f32),
            pltpu.VMEM((parts - 1, kept // rows, rows, 128), f32),
            pltpu.VMEM((parts - 1, kept // rows, rows, 128), f32),
            pltpu.VMEM((n, groups, rows, tile), f32),
            pltpu.VMEM((2, tiles, kept, tile), f32),
            pltpu.VMEM((parts - 1, 2, tiles, kept, tile), bf16),
            pltpu.VMEM((parts - 1, 2, tiles, kept, tile), bf16),
            dma((3,)),
            dma((2,)),
            dma((2,)),
            dma((parts, blocks)),
            dma((groups * n,)),
            dma((groups * n,)),
            dma((groups * n,)),
            dma((2, h, SUBS)),
            dma((2, h, SUBS)),
            dma((2, h, SUBS)),
            dma((2, h, SUBS)),
            dma((n, SUBS)),
            dma((n, SUBS)),
            dma((parts - 1,)),
            dma((parts - 1,)),
            dma((parts - 1, 2, tiles)),
            dma((parts - 1, 2, tiles)),
        ],
        compiler_params=pltpu.CompilerParams(
            collective_id=0, has_side_effects=True, vmem_limit_bytes=67043328
        ),
    )(attended, residual_in, out_weight, gate_weight, up_weight)


def body(
    queries,
    new_keys,
    new_values,
    key_cache,
    value_cache,
    context_len,
    cache_slot,
    residual_in,
    out_weight,
    gate_weight,
    up_weight,
):
    local_rows = queries.shape[0]
    row_base = lax.axis_index(("grp", "mr")) * local_rows
    device_slot_index = cache_slot - row_base
    positions = jnp.arange(local_rows, dtype=jnp.int32)
    matches = device_slot_index[:, None] == positions[None, :]
    inverse = jnp.sum(jnp.where(matches, positions[:, None], 0), axis=0)
    by_cache = attend_rows(
        jnp.take(queries, inverse, axis=0),
        jnp.take(new_keys, inverse, axis=0),
        jnp.take(new_values, inverse, axis=0),
        key_cache,
        value_cache,
        jnp.take(context_len, inverse, axis=0),
    )
    attended = jnp.take(by_cache, device_slot_index, axis=0)
    sizes = (lax.axis_size("grp"), lax.axis_size("mr"), lax.axis_size("mc"))
    return layer(sizes, attended, residual_in, out_weight, gate_weight, up_weight)


def solution(mesh):
    in_specs = (
        P(("grp", "mr"), "mc"),
        P(("grp", "mr"), "mc"),
        P(("grp", "mr"), "mc"),
        P(("grp", "mr"), None, "mc"),
        P(("grp", "mr"), None, "mc"),
        P(("grp", "mr")),
        P(("grp", "mr")),
        P(("grp", "mr"), "mc"),
        P(("grp", "mr"), "mc"),
        P("mc", ("grp", "mr")),
        P("mc", ("grp", "mr")),
    )
    out_specs = (P(("grp", "mr"), "mc"), P("mc", ("grp", "mr")))
    return jax.shard_map(body, mesh=mesh, in_specs=in_specs, out_specs=out_specs, check_vma=False)
```

time: 236 us -> 119 us (0.50)
  waiting for transfers between devices: 149 us -> 0 us
  Pallas kernels: 0 us -> 93.1 us
  matrix products: 36.3 us -> 12.4 us
  between operations: 14.3 us -> 0.76 us
  starting transfers between devices: 9.95 us -> 0 us
  blocking collectives: 8.53 us -> 0 us
  other arithmetic: 9.32 us -> 2.42 us
    pallas_call x0 -> x1, Pallas kernels: none -> 93.1 us  [layer(): pl.pallas_call(functools.partial(layer_kernel, sizes), out_shape=(jax.Sha...]
    reduce_scatter x1 -> x0, waiting for transfers between devices: 63.5 us -> none  [body(): lax.psum_scatter(own_share.astype(jnp.bfloat16), 'mr', scatter_dimension=...]
    all_gather x1 -> x0, waiting for transfers between devices: 44.1 us -> none  [body(): group_part = lax.all_gather(residual_out, 'mr', axis=0, tiled=True)]
    ppermute x5 -> x0, waiting for transfers between devices: 28.4 us -> none  [the longest x3 21.1 us: scatter_sum(): total = total + lax.ppermute(sent, 'mc', pairs).astype(jnp.float32)]
    dot_general x4 -> x0, matrix products: 23.9 us -> none  [the longest x1 9.31 us: body(): jnp.dot(everyone, gate_weight, preferred_element_type=jnp.float32)]
    all_to_all x1 -> x0, waiting for transfers between devices: 13 us -> none  [body(): lax.all_to_all(gathered, ('grp', 'mr'), split_axis=1, concat_axis=0, tile...]
    all_gather x1 -> x0, blocking collectives: 8.53 us -> none  [body(): gathered = lax.all_gather(attended, 'mc', axis=1, tiled=True)]
    all_to_all x1 -> x0, starting transfers between devices: 6.19 us -> none  [body(): lax.all_to_all(gathered, ('grp', 'mr'), split_axis=1, concat_axis=0, tile...]
  transfers between devices with their start and end apart: 8 -> 0, of which waited for: 6 -> 0; matrix products, arithmetic and copies ran while one was open for 3% -> 0% of each run, Pallas kernels for 0% -> 0%
where the time goes in v1:
time: 119 us
  Pallas kernels  93.1 us (78%)
  matrix products  12.4 us (10%)
  local copies, waits for them, and re-layouts  10.3 us (9%)
  other arithmetic  2.42 us (2%)
    pallas_call x1, Pallas kernels, layer(): pl.pallas_call(functools.partial(layer_kernel, sizes), out_shape=(jax.Sha...  93.1 us
    dot_general x1, matrix products, attend_rows(): jnp.einsum('bkgd,bckd->bkgc', query_grouped_four, key_four, preferred_ele...  6.45 us
    dot_general x1, matrix products, attend_rows(): jnp.einsum('bkgc,bckd->bkgd', weights, value_four, preferred_element_type...  5.76 us
    unnamed x4, local copies, waits for them, and re-layouts  3.72 us

profile of v1, /device:TPU:0, one launch (start us, length us, event | category | flops | bytes accessed | tf_op | source)
XLA Modules:
  0.0 119.0 jit_solution(14774721154969289261)
XLA Ops:
  0.6 0.7 compare_and_fusion
  1.3 0.1 select_reduce_fusion
  1.4 1.4 %gather_fusion = s32[24]{0:T(128)S(1)} fusion(s32[24]{0:T(128)} %param.20, s32[1024]{0:T(1024)S(1)} %pad_clamp_fusion.2), kind=kCustom, calls=%fused_computation.4 | custom fusion | bytes 288 | tf_op jit(solution)/shard_map/jit(_take)/gather | solution.py:526
  2.8 1.4 %gather_fusion.2 = bf16[24,512]{1,0:T(8,128)(2,1)S(1)} fusion(bf16[24,512]{1,0:T(8,128)(2,1)} %param.16, s32[1024]{0:T(1024)S(1)} %pad_clamp_fusion.1), kind=kCustom, calls=%fused_computation.1.clone | custom fusion | bytes 49248 | tf_op jit(solution)/shard_map/jit(_take)/gather | solution.py:522
  4.1 1.4 %gather_fusion.3 = bf16[24,512]{1,0:T(8,128)(2,1)S(1)} fusion(bf16[24,512]{1,0:T(8,128)(2,1)} %param.17, s32[1024]{0:T(1024)S(1)} %pad_clamp_fusion.1), kind=kCustom, calls=%fused_computation.3.clone | custom fusion | bytes 49248 | tf_op jit(solution)/shard_map/jit(_take)/gather | solution.py:523
  5.5 0.1 select_convert_fusion
  5.6 1.8 %gather_fusion.1 = bf16[24,4096]{1,0:T(8,128)(2,1)S(1)} fusion(bf16[24,4096]{1,0:T(8,128)(2,1)} %param.15, s32[1024]{0:T(1024)S(1)} %pad_clamp_fusion.1), kind=kCustom, calls=%fused_computation.clone | custom fusion | bytes 393312 | tf_op jit(solution)/shard_map/jit(_take)/gather | solution.py:521
  7.4 0.1 select_bitcast_fusion
  7.5 0.2 fusion.21
  7.8 0.1 iota_compare_fusion
  7.9 6.5 %fusion.20 = (f32[24,4,8]{2,1,0:T(4,128)S(1)}, f32[24,4,8,512]{3,2,1,0:T(8,128)S(1)}) fusion(bf16[24,4,8,128]{3,2,1,0:T(8,128)(2,1)S(1)} %bitcast.42, pred[24,512]{1,0:T(8,128)(4,1)S(1)} %iota_compare_fusion, bf16[24,512,512]{2,1,0:T(8,128)(2,1)} %param.18), kind=kOutput, calls=%fused_computation.43 | convolution fusion | flops 101842176 | bytes 14367744 | tf_op jit(solution)/shard_map/bkgd,bckd->bkgc/dot_general | solution.py:30
  14.4 0.6 fusion.8
  15.0 5.8 %fusion.12 = bf16[24,4,8,128]{3,2,1,0:T(8,128)(2,1)S(1)} fusion(f32[24,4,8,512]{3,2,1,0:T(8,128)S(1)} %get-tuple-element.14, f32[24,4,8]{2,1,0:T(4,128)S(1)} %get-tuple-element.9, f32[24,4,8]{2,1,0:T(4,128)S(1)} %multiply_maximum_fusion, f32[24,4,128]{2,1,0:T(4,128)S(1)} %reshape.87, f32[24,4,8]{2,1,0:T(4,128)S(1)} %get-tuple-element.8, ...), kind=kOutput, calls=%fused_computation.16 | convolution fusion | flops 102137856 | bytes 14410752 | tf_op jit(solution)/shard_map/bkgc,bckd->bkgd/dot_general | solution.py:50
  20.8 0.1 copy.42
  20.9 0.7 gather_fusion.4
  21.5 0.8 broadcast_select_fusion.att
  22.3 93.1 %shard_map.122 = (bf16[24,4096]{1,0:T(8,128)(2,1)}, bf16[192,1792]{1,0:T(8,128)(2,1)}) custom-call(bf16[24,4096]{1,0:T(8,128)(2,1)} %broadcast_select_fusion.att, bf16[24,4096]{1,0:T(8,128)(2,1)} %res_in.1, bf16[512,4096]{1,0:T(8,128)(2,1)} %w_hbm.1, bf16[4096,1792]{1,0:T(8,128)(2,1)} %gate_hbm.1, bf16[4096,1792]{1,0:T(8,128)(2,1)} %up_hbm.1), custom_call_target="tpu_custom_call" | custom-call | tf_op jit(solution)/shard_map/pallas_call | solution.py:451
  115.4 1.6 %copy.45 = bf16[24,4096]{1,0:T(8,128)(2,1)} copy(bf16[24,4096]{1,0:T(8,128)(2,1)} %get-tuple-element.17) | data formatting | bytes 393216
  117.1 2.0 %copy.46 = bf16[192,1792]{1,0:T(8,128)(2,1)} copy(bf16[192,1792]{1,0:T(8,128)(2,1)} %get-tuple-element.18) | data formatting | bytes 1376256
  (11 shorter events, 0.2 us)

commit v2 on v1

v2 whole, which is shorter than its diff:
```python
import functools

import jax
import jax.numpy as jnp
from jax import lax
from jax.experimental import pallas as pl
from jax.experimental.pallas import tpu as pltpu
from jax.sharding import PartitionSpec as P

D = 8192
HD = 128


norm_epsilon = 1e-05
masked_score = -1e30


SPANS = 2
BATCH = 6
AHEAD = 3


def attend_kernel(
    lengths,
    slots,
    queries,
    new_keys,
    new_values,
    key_hbm,
    value_hbm,
    out,
    keys,
    values,
    by_head,
    out_head,
    own_keys,
    own_values,
    held,
    own_held,
    key_sem,
    value_sem,
):
    rows = queries.shape[0]
    context, width = keys.shape[1:]
    kv_heads = width // HD
    heads = queries.shape[1] // HD
    groups = heads // kv_heads
    span = context // SPANS
    scale = HD ** (-0.5)
    base = (lax.axis_index("grp") * lax.axis_size("mr") + lax.axis_index("mr")) * rows

    def copy(which, r, b):
        hbm, buffer, sem = (
            (key_hbm, keys, key_sem) if which == 0 else (value_hbm, values, value_sem)
        )
        positions = pl.ds(b * span, span)
        return pltpu.make_async_copy(
            hbm.at[slots[r] - base, positions], buffer.at[r, positions], sem.at[r, b]
        )

    def when_used(r, b, act):
        if b == 0:
            act()
        else:
            pl.when(lengths[r] > b * span)(act)

    def fetch(batch):
        for which in range(2):
            for i in range(BATCH):
                r = batch * BATCH + i
                for b in range(SPANS):
                    when_used(r, b, lambda: copy(which, r, b).start())
        for i in range(BATCH):
            r = batch * BATCH + i
            for b in range(1, SPANS):

                @pl.when(lengths[r] <= b * span)
                def _():
                    values[r, b * span : (b + 1) * span] = jnp.zeros((span, width), values.dtype)

    row_head = lax.broadcasted_iota(jnp.int32, (heads, width), 0) // groups
    column_head = lax.broadcasted_iota(jnp.int32, (heads, width), 1) // HD
    same_head = row_head == column_head

    def weigh(r):
        length = lengths[r]
        query = by_head[pl.ds(r, heads, stride=rows), :]
        spread = jnp.where(same_head, jnp.concatenate([query] * kv_heads, axis=1), 0.0)
        scores = (
            lax.dot_general(
                spread.astype(jnp.bfloat16),
                keys[r],
                (((1,), (1,)), ((), ())),
                preferred_element_type=jnp.float32,
            )
            * scale
        )
        positions = lax.broadcasted_iota(jnp.int32, (heads, context), 1)
        scores = jnp.where(positions < length, scores, masked_score)
        own_score = jnp.sum(spread * own_keys[pl.ds(r, 1), :], axis=1, keepdims=True) * scale
        top = jnp.maximum(jnp.max(scores, axis=1, keepdims=True), own_score)
        exponent = jnp.exp(scores - top)
        own_exponent = jnp.exp(own_score - top)
        denominator = jnp.sum(exponent, axis=1, keepdims=True) + own_exponent
        weights = (exponent / denominator).astype(jnp.bfloat16)
        own_weight = (own_exponent / denominator).astype(jnp.bfloat16).astype(jnp.float32)
        return weights, jnp.broadcast_to(own_weight, (heads, HD))

    def combine(r, weights, own_weight):
        combined = jnp.dot(weights, values[r], preferred_element_type=jnp.float32)
        combined = combined + own_weight[:, :1] * own_values[pl.ds(r, 1), :]
        combined = jnp.where(same_head, combined, 0.0)
        picked = combined[:, :HD]
        for k in range(1, kv_heads):
            picked = picked + combined[:, k * HD : (k + 1) * HD]
        return picked

    def weigh_batch(batch):
        return [weigh(batch * BATCH + i) for i in range(BATCH)]

    def hold(found):
        for i, (weights, own_weight) in enumerate(found):
            held[i] = weights
            own_held[i] = own_weight

    def combine_batch(batch):
        return [combine(batch * BATCH + i, held[i], own_held[i]) for i in range(BATCH)]

    def put(batch, picked):
        for i in range(BATCH):
            out_head[pl.ds(batch * BATCH + i, heads, stride=rows), :] = picked[i]

    def arrive(which, batch):
        for i in range(BATCH):
            r = batch * BATCH + i
            for b in range(SPANS):
                when_used(r, b, lambda: copy(which, r, b).wait())

    batches = rows // BATCH

    def first(batch, carry):
        fetch(batch)
        return carry

    lax.fori_loop(0, min(AHEAD, batches), first, 0)

    own_keys[...] = new_keys[...].astype(jnp.float32)
    own_values[...] = new_values[...].astype(jnp.float32)
    for j in range(heads):
        by_head[j * rows : (j + 1) * rows, :] = queries[:, j * HD : (j + 1) * HD].astype(
            jnp.float32
        )

    arrive(0, 0)
    hold(weigh_batch(0))

    def step(batch, carry):
        @pl.when(batch + AHEAD <= batches)
        def _():
            fetch(batch + AHEAD - 1)

        arrive(1, batch - 1)
        arrive(0, batch)
        picked = combine_batch(batch - 1)
        found = weigh_batch(batch)
        put(batch - 1, picked)
        hold(found)
        return carry

    lax.fori_loop(1, batches, step, 0)
    arrive(1, batches - 1)
    put(batches - 1, combine_batch(batches - 1))
    for j in range(heads):
        out[:, j * HD : (j + 1) * HD] = out_head[j * rows : (j + 1) * rows, :].astype(jnp.bfloat16)


def attend_rows(queries, new_keys, new_values, key_cache, value_cache, context_len, cache_slot):
    rows = queries.shape[0]
    _, context, width = key_cache.shape
    heads = queries.shape[1] // HD
    vmem = pl.BlockSpec(memory_space=pltpu.VMEM)
    smem = pl.BlockSpec(memory_space=pltpu.SMEM)
    hbm = pl.BlockSpec(memory_space=pltpu.HBM)
    return pl.pallas_call(
        attend_kernel,
        out_shape=jax.ShapeDtypeStruct(queries.shape, jnp.bfloat16),
        in_specs=[smem, smem, vmem, vmem, vmem, hbm, hbm],
        out_specs=vmem,
        scratch_shapes=[
            pltpu.VMEM((rows, context, width), jnp.bfloat16),
            pltpu.VMEM((rows, context, width), jnp.bfloat16),
            pltpu.VMEM((heads * rows, HD), jnp.float32),
            pltpu.VMEM((heads * rows, HD), jnp.float32),
            pltpu.VMEM((rows, width), jnp.float32),
            pltpu.VMEM((rows, width), jnp.float32),
            pltpu.VMEM((BATCH, heads, context), jnp.bfloat16),
            pltpu.VMEM((BATCH, heads, HD), jnp.float32),
            pltpu.SemaphoreType.DMA((rows, SPANS)),
            pltpu.SemaphoreType.DMA((rows, SPANS)),
        ],
        compiler_params=pltpu.CompilerParams(vmem_limit_bytes=56 * 1024 * 1024),
    )(context_len, cache_slot, queries, new_keys, new_values, key_cache, value_cache)


MESH = pl.DeviceIdType.MESH
SUBS = 4


def remote(src, dst, send_sem, recv_sem, device):
    return pltpu.make_async_remote_copy(
        src_ref=src,
        dst_ref=dst,
        send_sem=send_sem,
        recv_sem=recv_sem,
        device_id=device,
        device_id_type=MESH,
    )


def layer_kernel(
    sizes,
    att_hbm,
    res_hbm,
    w_hbm,
    gate_hbm,
    up_hbm,
    res_out_hbm,
    act_out_hbm,
    att,
    res_in,
    res_out,
    act_out,
    w_buf,
    gate_buf,
    up_buf,
    res_peer,
    disp,
    feats,
    acc,
    rs_send,
    rs_recv,
    xg,
    squares,
    sq_keep,
    sq_send,
    sq_recv,
    result,
    keep,
    ex_send,
    ex_recv,
    load_sem,
    store_sem,
    peer_send_sem,
    peer_recv_sem,
    disp_send_sem,
    disp_recv_sem,
    fwd_send_sem,
    fwd_recv_sem,
    rs_send_sem,
    rs_recv_sem,
    ag_send_sem,
    ag_recv_sem,
    half_send_sem,
    half_recv_sem,
    sq_send_sem,
    sq_recv_sem,
    ex_send_sem,
    ex_recv_sem,
):
    groups, n, parts = sizes
    h = n // 2
    g = lax.axis_index("grp")
    m = lax.axis_index("mr")
    c = lax.axis_index("mc")
    peer = (1 - g, m, c)
    rows, width = att.shape
    feat = w_hbm.shape[0]
    half = width // 2
    sub = half // SUBS
    blocks = width // feat
    tile = result.shape[4]
    tiles = act_out.shape[2] // tile

    def chip_at(q):
        q = lax.rem(q + 2 * n, n)
        t = q // h
        return (1 - t) * 2 * q + t * (2 * n - 1 - 2 * q)

    place = (1 - m % 2) * (m // 2) + (m % 2) * (n - 1 - m // 2)
    right = (g, chip_at(place + 1), c)
    left = (g, chip_at(place - 1), c)

    w_load = pltpu.make_async_copy(
        w_hbm.at[:, pl.ds(pl.multiple_of(g * half, half), half)], w_buf.at[g], load_sem.at[0]
    )
    gate_load = pltpu.make_async_copy(gate_hbm, gate_buf, load_sem.at[1])
    up_load = pltpu.make_async_copy(up_hbm, up_buf, load_sem.at[2])
    att_load = pltpu.make_async_copy(att_hbm, att, load_sem.at[3])
    res_load = pltpu.make_async_copy(res_hbm, res_in, load_sem.at[4])
    att_load.start()
    res_load.start()
    w_load.start()

    barrier = pltpu.get_barrier_semaphore()
    total = groups * n * parts
    me = (g * n + m) * parts + c

    def greet(i, carry):
        other = lax.rem(me + i, total)
        device = (other // (n * parts), (other // parts) % n, other % parts)
        pl.semaphore_signal(barrier, inc=1, device_id=device, device_id_type=MESH)
        return carry

    lax.fori_loop(1, total, greet, 0)
    pl.semaphore_wait(barrier, total - 1)

    pending = []
    own_slot = g * n + m
    att_load.wait()
    res_load.wait()

    for k in range(parts):
        for j in range(blocks):
            jj = lax.rem(m + j, blocks)
            block = c * blocks + jj
            device = (block // n, block % n, lax.rem(c + k, parts))
            copy = remote(
                att.at[:, pl.ds(pl.multiple_of(jj * feat, feat), feat)],
                disp.at[block // n, own_slot],
                disp_send_sem.at[k, j],
                disp_recv_sem.at[own_slot],
                device,
            )
            if k == 0:
                pl.when(block != own_slot)(copy.start)

                @pl.when(block == own_slot)
                def _():
                    disp[g, own_slot] = att[:, pl.ds(pl.multiple_of(jj * feat, feat), feat)]

                pending.append((copy, block != own_slot))
            else:
                copy.start()
                pending.append((copy, None))

    other_cols = pl.ds(pl.multiple_of((1 - g) * half, half), half)
    own_cols = pl.ds(pl.multiple_of(g * half, half), half)
    w_share = remote(
        w_hbm.at[:, other_cols], w_buf.at[g], peer_send_sem.at[0], peer_recv_sem.at[0], peer
    )
    w_share.start()
    res_share = remote(
        res_in.at[:, other_cols], res_peer, peer_send_sem.at[1], peer_recv_sem.at[1], peer
    )
    res_share.start()
    pending += [(w_share, None), (res_share, None)]
    gate_load.start()
    up_load.start()

    source = own_slot // blocks
    from_self = c == source
    for i in range(groups * n):
        arrived = remote(
            disp.at[g, i], disp.at[g, i], disp_send_sem.at[0, 0], disp_recv_sem.at[i], peer
        )
        is_remote = jnp.logical_or(source != c, own_slot != i)
        pl.when(is_remote)(arrived.wait_recv)
        forward = remote(
            disp.at[g, i], disp.at[g, i], fwd_send_sem.at[i], fwd_recv_sem.at[i], peer
        )
        forward.start()
        pending.append((forward, None))
    for i in range(groups * n):
        remote(
            disp.at[1 - g, i], disp.at[1 - g, i], fwd_send_sem.at[i], fwd_recv_sem.at[i], peer
        ).wait_recv()
    for i in range(n):
        for k in range(groups):
            pair = [disp[k, gg * n + i].astype(jnp.float32) for gg in range(groups)]
            feats[i, :, k * feat : (k + 1) * feat] = jnp.concatenate(pair, axis=0).astype(
                jnp.bfloat16
            )
    w_load.wait()
    w_share.wait_recv()
    res_share.wait_recv()

    step_cols = min(512, half)

    def project(t, carry):
        cols = pl.ds(pl.multiple_of(t * step_cols, step_cols), step_cols)
        value = jnp.dot(
            feats[...].reshape(n * groups * rows, groups * feat),
            w_buf[:, :, cols].reshape(groups * feat, step_cols),
            preferred_element_type=jnp.float32,
        )
        acc[:, :, cols] = value.reshape(n, groups * rows, step_cols)
        return carry

    lax.fori_loop(0, half // step_cols, project, 0)

    def travels(direction, k):
        return (k < SUBS // 2) == (direction == 0)

    def rs_copy(direction, s, k):
        cols = pl.ds(k * sub, sub)
        return remote(
            rs_send.at[direction, s, :, cols],
            rs_recv.at[direction, s, :, cols],
            rs_send_sem.at[direction, s, k],
            rs_recv_sem.at[direction, s, k],
            right if direction == 0 else left,
        )

    for s in range(h):
        for turn in range(SUBS):
            for direction in range(2):
                k = (turn + SUBS // 2) % SUBS if direction == 0 else turn
                if s == 0 and not travels(direction, k):
                    continue
                cols = pl.ds(k * sub, sub)
                goal = chip_at(place + h - s if direction == 0 else place - h + s)
                value = acc[goal, :, cols]
                if s > 1 or (s == 1 and travels(direction, k)):
                    rs_copy(direction, s - 1, k).wait_recv()
                    value = value + rs_recv[direction, s - 1, :, cols].astype(jnp.float32)
                rs_send[direction, s, :, cols] = value.astype(jnp.bfloat16)
                copy = rs_copy(direction, s, k)
                copy.start()
                pending.append((copy, None))

    def ag_copy(direction, s, k, holder):
        cols = pl.ds(pl.multiple_of(g * half + k * sub, sub), sub)
        return remote(
            xg.at[holder, :, cols],
            xg.at[holder, :, cols],
            ag_send_sem.at[direction, s, k],
            ag_recv_sem.at[direction, s, k],
            right if direction == 0 else left,
        )

    def half_copy(holder, side, slot, k):
        cols = pl.ds(pl.multiple_of(side * half + k * sub, sub), sub)
        return remote(
            xg.at[holder, :, cols],
            xg.at[holder, :, cols],
            half_send_sem.at[slot, k],
            half_recv_sem.at[slot, k],
            peer,
        )

    for k in range(SUBS):
        cols = pl.ds(k * sub, sub)
        mine = res_in[:, pl.ds(pl.multiple_of(g * half + k * sub, sub), sub)].astype(jnp.float32)
        other = res_peer[:, cols].astype(jnp.float32)
        first = jnp.where(g == 0, mine, other)
        second = jnp.where(g == 0, other, mine)
        value = acc[m, :, cols] + jnp.concatenate([first, second], axis=0)
        for direction in range(2):
            rs_copy(direction, h - 1, k).wait_recv()
            value = value + rs_recv[direction, h - 1, :, cols].astype(jnp.float32)
        xg[m, :, pl.ds(pl.multiple_of(g * half + k * sub, sub), sub)] = value.astype(jnp.bfloat16)
        copy = half_copy(m, g, 0, k)
        copy.start()
        pending.append((copy, None))
        if h > 1 or travels(0, k):
            copy = ag_copy(0, 0, k, m)
            copy.start()
            pending.append((copy, None))

    for turn in range(SUBS):
        k = (turn + SUBS // 2) % SUBS
        if h > 1 or travels(1, k):
            copy = ag_copy(1, 0, k, m)
            copy.start()
            pending.append((copy, None))

    order = [m]
    for s in range(h - 1):
        order += [chip_at(place - 1 - s), chip_at(place + 1 + s)]
    order.append(chip_at(place + h))
    stages = [(0, 1)] + [(1 + 2 * s, 2) for s in range(h - 1)] + [(n - 1, 1)]
    per_group = parts // groups
    count = n // per_group
    own_group = c // per_group

    def keeper(group, holder):
        return group * per_group + holder // count

    def slot_of(source, target):
        return 0 if parts == 2 else lax.rem(source - target + parts, parts) - 1

    def ex_copy(source, target, stage, t):
        first, size = stage
        where = (slot_of(source, target), t, slice(None), pl.ds(first, size))
        return remote(
            ex_send.at[where],
            ex_recv.at[where],
            ex_send_sem.at[slot_of(source, target), t, first],
            ex_recv_sem.at[slot_of(source, target), t, first],
            (g, m, target),
        )

    def sq_copy(source, target, stage):
        first, size = stage
        where = (slot_of(source, target), pl.ds(first, size))
        return remote(
            sq_send.at[where],
            sq_recv.at[where],
            sq_send_sem.at[slot_of(source, target), first],
            sq_recv_sem.at[slot_of(source, target), first],
            (g, m, target),
        )

    def items(stage):
        first, size = stage
        if per_group == 1:
            return [stage]
        return [(first + i, 1) for i in range(size)]

    def mine_to_keep(j, item):
        if j > 0:
            return False, None
        if per_group == 1:
            return True, None
        return None, order[item[0]] // count == lax.rem(c, per_group)

    def pack_squares(column):
        lane = lax.broadcasted_iota(jnp.int32, (8, 128), 1)
        packed = jnp.zeros((8, 128), jnp.float32)
        for a in range(rows // 8):
            packed = packed + jnp.where(lane == a, column[8 * a : 8 * a + 8], 0.0)
        return packed

    def route(j, item, keep_it, send_it):
        certain, condition = mine_to_keep(j, item)
        if certain is None:
            pl.when(condition)(keep_it)
            pl.when(jnp.logical_not(condition))(send_it)
        elif certain:
            keep_it()
        else:
            send_it()

    def run_stage(stage):
        first, size = stage
        for i in range(first, first + size):
            wide = xg[order[i]].astype(jnp.float32)
            summed = jnp.sum(wide * wide, axis=1, keepdims=True)
            squares[i] = jnp.broadcast_to(summed, (groups * rows, 128)).reshape(groups, rows, 128)
        for item in items(stage):
            for j in range(groups):
                group = lax.rem(own_group + j, groups)
                target = keeper(group, order[item[0]])

                def keep_it(item=item, group=group):
                    for i in range(item[0], item[0] + item[1]):
                        sq_keep[i] = pack_squares(squares[i, group])

                def send_it(item=item, group=group, target=target):
                    for i in range(item[0], item[0] + item[1]):
                        sq_send[slot_of(c, target), i] = pack_squares(squares[i, group])
                    sq_copy(c, target, item).start()

                route(j, item, keep_it, send_it)

        def expand(t, carry):
            cols = pl.ds(pl.multiple_of(t * tile, tile), tile)
            lhs = jnp.concatenate([xg[order[i]] for i in range(first, first + size)], axis=0)
            for w, weights in enumerate((gate_buf, up_buf)):
                value = jnp.dot(lhs, weights[:, cols], preferred_element_type=jnp.float32)
                result[w, :size] = value.reshape(size, groups, rows, tile)
            for item in items(stage):
                local = pl.ds(item[0] - first, item[1])
                for j in range(groups):
                    group = lax.rem(own_group + j, groups)
                    target = keeper(group, order[item[0]])

                    def keep_it(item=item, local=local, group=group):
                        keep[t, :, pl.ds(item[0], item[1])] = result[:, local, group]

                    def send_it(item=item, local=local, group=group, target=target):
                        ex_send[slot_of(c, target), t, :, pl.ds(item[0], item[1])] = result[
                            :, local, group
                        ].astype(jnp.bfloat16)
                        ex_copy(c, target, item, t).start()

                    route(j, item, keep_it, send_it)
            return carry

        lax.fori_loop(0, tiles, expand, 0)

    gate_load.wait()
    up_load.wait()
    res_store = pltpu.make_async_copy(res_out, res_out_hbm, load_sem.at[5])
    for s in range(-1, h):
        for turn in range(SUBS):
            if s < 0:
                break
            for direction in range(2):
                k = turn if direction == 0 else (turn + SUBS // 2) % SUBS
                last = s == h - 1
                if last and not travels(direction, k):
                    continue
                holder = chip_at(place - 1 - s if direction == 0 else place + 1 + s)
                slot = n - 1 if last else 1 + 2 * s + direction
                ag_copy(direction, s, k, holder).wait_recv()
                if s + 1 < h and (s + 1 < h - 1 or travels(direction, k)):
                    copy = ag_copy(direction, s + 1, k, holder)
                    copy.start()
                    pending.append((copy, None))
                copy = half_copy(holder, g, slot, k)
                copy.start()
                pending.append((copy, None))
        stage = stages[s + 1]
        for i in range(stage[0], stage[0] + stage[1]):
            for k in range(SUBS):
                half_copy(order[i], 1 - g, i, k).wait_recv()
        if s < 0:
            both = xg[m].astype(jnp.float32)
            res_out[...] = jnp.where(g == 0, both[:rows], both[rows:]).astype(jnp.bfloat16)
            res_store.start()
        run_stage(stage)

    def finish(item):
        total = [sq_keep[i] for i in range(item[0], item[0] + item[1])]
        for k in range(1, parts):
            source = lax.rem(c + k, parts)
            sq_copy(source, c, item).wait_recv()
            total = [
                value + sq_recv[slot_of(source, c), item[0] + i] for i, value in enumerate(total)
            ]
        inverse = []
        for value in total:
            packed = lax.rsqrt(value / D + norm_epsilon)
            inverse.append(
                jnp.concatenate([packed[:, a : a + 1] for a in range(rows // 8)], axis=0)
            )

        def activate(t, carry):
            for k in range(1, parts):
                ex_copy(lax.rem(c + k, parts), c, item, t).wait_recv()
            cols = pl.ds(pl.multiple_of(t * tile, tile), tile)
            for i, scale in enumerate(inverse):
                sums = []
                for w in range(2):
                    value = keep[t, w, item[0] + i]
                    for k in range(1, parts):
                        slot = slot_of(lax.rem(c + k, parts), c)
                        value = value + ex_recv[slot, t, w, item[0] + i].astype(jnp.float32)
                    sums.append(value * scale)
                gate, up = sums
                holder = order[item[0] + i]
                act_out[lax.rem(holder, count), :, cols] = (
                    gate / (1.0 + jnp.exp(-gate)) * up
                ).astype(jnp.bfloat16)
            return carry

        lax.fori_loop(0, tiles, activate, 0)
        for i in range(item[0], item[0] + item[1]):
            store(lax.rem(order[i], count)).start()

    def store(index):
        return pltpu.make_async_copy(
            act_out.at[index], act_out_hbm.at[index], store_sem.at[index]
        )

    def sent(item, target):
        sq_copy(c, target, item).wait_send()

        def each(t, carry):
            ex_copy(c, target, item, t).wait_send()
            return carry

        lax.fori_loop(0, tiles, each, 0)

    for stage in stages:
        for item in items(stage):
            route(0, item, functools.partial(finish, item), lambda: None)
            for j in range(groups):
                target = keeper(lax.rem(own_group + j, groups), order[item[0]])
                route(j, item, lambda: None, functools.partial(sent, item, target))

    res_store.wait()
    for i in range(count):
        store(i).wait()
    for copy, condition in pending:
        if condition is None:
            copy.wait_send()
        else:
            pl.when(condition)(copy.wait_send)


def layer(sizes, attended, residual_in, out_weight, gate_weight, up_weight):
    groups, n, parts = sizes
    h = n // 2
    rows, width = attended.shape
    feat = out_weight.shape[0]
    half = width // 2
    hidden = gate_weight.shape[1]
    tile = hidden // 2 if hidden % 256 == 0 else 128
    tiles = hidden // tile
    kept = groups * n * rows // parts
    bf16, f32 = jnp.bfloat16, jnp.float32
    dma = pltpu.SemaphoreType.DMA
    hbm = pl.BlockSpec(memory_space=pltpu.HBM)
    blocks = width // feat
    residual_out, activation = pl.pallas_call(
        functools.partial(layer_kernel, sizes),
        out_shape=(
            jax.ShapeDtypeStruct((rows, width), bf16),
            jax.ShapeDtypeStruct((kept // rows, rows, hidden), bf16),
        ),
        in_specs=[hbm] * 5,
        out_specs=(hbm, hbm),
        scratch_shapes=[
            pltpu.VMEM((rows, width), bf16),
            pltpu.VMEM((rows, width), bf16),
            pltpu.VMEM((rows, width), bf16),
            pltpu.VMEM((kept // rows, rows, hidden), bf16),
            pltpu.VMEM((groups, feat, half), bf16),
            pltpu.VMEM(gate_weight.shape, bf16),
            pltpu.VMEM(up_weight.shape, bf16),
            pltpu.VMEM((rows, half), bf16),
            pltpu.VMEM((groups, groups * n, rows, feat), bf16),
            pltpu.VMEM((n, groups * rows, groups * feat), bf16),
            pltpu.VMEM((n, groups * rows, half), f32),
            pltpu.VMEM((2, h, groups * rows, half), bf16),
            pltpu.VMEM((2, h, groups * rows, half), bf16),
            pltpu.VMEM((n, groups * rows, width), bf16),
            pltpu.VMEM((n, groups, rows, 128), f32),
            pltpu.VMEM((n, 8, 128), f32),
            pltpu.VMEM((parts - 1, n, 8, 128), f32),
            pltpu.VMEM((parts - 1, n, 8, 128), f32),
            pltpu.VMEM((2, 2, groups, rows, tile), f32),
            pltpu.VMEM((tiles, 2, n, rows, tile), f32),
            pltpu.VMEM((parts - 1, tiles, 2, n, rows, tile), bf16),
            pltpu.VMEM((parts - 1, tiles, 2, n, rows, tile), bf16),
            dma((6,)),
            dma((kept // rows,)),
            dma((2,)),
            dma((2,)),
            dma((parts, blocks)),
            dma((groups * n,)),
            dma((groups * n,)),
            dma((groups * n,)),
            dma((2, h, SUBS)),
            dma((2, h, SUBS)),
            dma((2, h, SUBS)),
            dma((2, h, SUBS)),
            dma((n, SUBS)),
            dma((n, SUBS)),
            dma((parts - 1, n)),
            dma((parts - 1, n)),
            dma((parts - 1, tiles, n)),
            dma((parts - 1, tiles, n)),
        ],
        compiler_params=pltpu.CompilerParams(
            collective_id=0, has_side_effects=True, vmem_limit_bytes=56 * 1024 * 1024
        ),
    )(attended, residual_in, out_weight, gate_weight, up_weight)
    residual_out, activation = hand_over(residual_out, activation)
    return residual_out, activation.reshape(kept, hidden)


def hand_over_kernel(res_in, act_in, res_out, act_out, res_buf, act_buf, in_sem, out_sem):
    chips = act_in.shape[0]
    moves = [
        (
            pltpu.make_async_copy(res_in, res_buf, in_sem.at[chips]),
            pltpu.make_async_copy(res_buf, res_out, out_sem.at[chips]),
        )
    ]
    for i in range(chips):
        moves.append(
            (
                pltpu.make_async_copy(act_in.at[i], act_buf.at[i], in_sem.at[i]),
                pltpu.make_async_copy(act_buf.at[i], act_out.at[i], out_sem.at[i]),
            )
        )
    for into, _ in moves:
        into.start()
    for into, out in moves:
        into.wait()
        out.start()
    for _, out in moves:
        out.wait()


def hand_over(residual_out, activation):
    hbm = pl.BlockSpec(memory_space=pltpu.HBM)
    dma = pltpu.SemaphoreType.DMA((activation.shape[0] + 1,))
    return pl.pallas_call(
        hand_over_kernel,
        out_shape=tuple(
            jax.ShapeDtypeStruct(x.shape, x.dtype) for x in (residual_out, activation)
        ),
        in_specs=[hbm, hbm],
        out_specs=(hbm, hbm),
        scratch_shapes=[
            pltpu.VMEM(residual_out.shape, residual_out.dtype),
            pltpu.VMEM(activation.shape, activation.dtype),
            dma,
            dma,
        ],
        compiler_params=pltpu.CompilerParams(vmem_limit_bytes=56 * 1024 * 1024),
    )(residual_out, activation)


def body(
    queries,
    new_keys,
    new_values,
    key_cache,
    value_cache,
    context_len,
    cache_slot,
    residual_in,
    out_weight,
    gate_weight,
    up_weight,
):
    attended = attend_rows(
        queries, new_keys, new_values, key_cache, value_cache, context_len, cache_slot
    )
    sizes = (lax.axis_size("grp"), lax.axis_size("mr"), lax.axis_size("mc"))
    return layer(sizes, attended, residual_in, out_weight, gate_weight, up_weight)


def solution(mesh):
    in_specs = (
        P(("grp", "mr"), "mc"),
        P(("grp", "mr"), "mc"),
        P(("grp", "mr"), "mc"),
        P(("grp", "mr"), None, "mc"),
        P(("grp", "mr"), None, "mc"),
        P(("grp", "mr")),
        P(("grp", "mr")),
        P(("grp", "mr"), "mc"),
        P(("grp", "mr"), "mc"),
        P("mc", ("grp", "mr")),
        P("mc", ("grp", "mr")),
    )
    out_specs = (P(("grp", "mr"), "mc"), P("mc", ("grp", "mr")))
    return jax.shard_map(body, mesh=mesh, in_specs=in_specs, out_specs=out_specs, check_vma=False)
```

time: 119 us -> 95.3 us (0.80)
  matrix products: 12.4 us -> 0 us
  local copies, waits for them, and re-layouts: 10.3 us -> 0 us
  other arithmetic: 2.42 us -> 0 us
  Pallas kernels: 93.1 us -> 94.3 us
    pallas_call x0 -> x2, Pallas kernels: none -> 14.4 us  [the longest x1 12.3 us: attend_rows(): pl.pallas_call(attend_kernel, out_shape=jax.ShapeDtypeStruct(queries.shap...]
    pallas_call x1, Pallas kernels: 93.1 us -> 80 us  [layer(): pl.pallas_call(functools.partial(layer_kernel, sizes), out_shape=(jax.Sha...]
    dot_general x3 -> x0, matrix products: 12.4 us -> none  [the longest x1 6.45 us: attend_rows(): jnp.einsum('bkgd,bckd->bkgc', query_grouped_four, key_four, preferred_ele...]
    gather x5 -> x0, local copies, waits for them, and re-layouts: 6.53 us -> none  [the longest x1 1.8 us: body(): jnp.take(queries, inverse, axis=0)]
    unnamed x4 -> x0, local copies, waits for them, and re-layouts: 3.72 us -> none
where the time goes in v2:
time: 95.3 us; the launch traced here: 95.2 us
  Pallas kernels  94.3 us (99%)
    pallas_call x1, Pallas kernels, layer(): pl.pallas_call(functools.partial(layer_kernel, sizes), out_shape=(jax.Sha...  80 us
    pallas_call x1, Pallas kernels, attend_rows(): pl.pallas_call(attend_kernel, out_shape=jax.ShapeDtypeStruct(queries.shap...  12.3 us
    pallas_call x1, Pallas kernels, hand_over(): pl.pallas_call(hand_over_kernel, out_shape=tuple((jax.ShapeDtypeStruct(x....  2.04 us

profile of v2, /device:TPU:0, one launch (start us, length us, event | category | flops | bytes accessed | tf_op | source)
XLA Modules:
  0.0 95.2 jit_solution(4895441118548627219)
XLA Ops:
  0.6 12.3 %shard_map.122.att_hbm = bf16[24,4096]{1,0:T(8,128)(2,1)} custom-call(s32[24]{0:T(128)} %lengths.1, s32[24]{0:T(128)} %slots.1, bf16[24,4096]{1,0:T(8,128)(2,1)} %queries.1, bf16[24,512]{1,0:T(8,128)(2,1)} %new_keys.1, bf16[24,512]{1,0:T(8,128)(2,1)} %new_values.1, bf16[24,512,512]{2,1,0:T(8,128)(2,1)} %key_hbm.1, bf16[24,512,512]{2,1,0:T(8,128)(2,1)} %value_hbm.1), custom_call_target="tpu_custom_call" | custom-call | tf_op jit(solution)/shard_map/pallas_call | solution.py:184
  13.0 80.0 %shard_map.123 = (bf16[24,4096]{1,0:T(8,128)(2,1)}, bf16[8,24,1792]{2,1,0:T(8,128)(2,1)}) custom-call(bf16[24,4096]{1,0:T(8,128)(2,1)} %shard_map.122.att_hbm, bf16[24,4096]{1,0:T(8,128)(2,1)} %res_hbm.1, bf16[512,4096]{1,0:T(8,128)(2,1)} %w_hbm.1, bf16[4096,1792]{1,0:T(8,128)(2,1)} %gate_hbm.1, bf16[4096,1792]{1,0:T(8,128)(2,1)} %up_hbm.1), custom_call_target="tpu_custom_call" | custom-call | tf_op jit(solution)/shard_map/pallas_call | solution.py:707
  92.9 2.0 %shard_map.124 = (bf16[24,4096]{1,0:T(8,128)(2,1)}, bf16[8,24,1792]{2,1,0:T(8,128)(2,1)}) custom-call(bf16[24,4096]{1,0:T(8,128)(2,1)} %get-tuple-element.6.res_in, bf16[8,24,1792]{2,1,0:T(8,128)(2,1)} %get-tuple-element.7.act_in), custom_call_target="tpu_custom_call" | custom-call | tf_op jit(solution)/shard_map/pallas_call | solution.py:792

commit v3 on v2

--- a/solution.py
+++ b/solution.py
@@ -215,6 +215,10 @@
         device_id=device,
         device_id_type=MESH,
     )
+
+
+def outward(count):
+    return [(d + 1) // 2 if d % 2 else count - d // 2 for d in range(count)]
 
 
 def layer_kernel(
@@ -319,9 +323,9 @@
     att_load.wait()
     res_load.wait()
 
-    for k in range(parts):
-        for j in range(blocks):
-            jj = lax.rem(m + j, blocks)
+    for j in range(blocks):
+        for k in range(parts):
+            jj = lax.rem(m + outward(blocks)[blocks - 1 - j], blocks)
             block = c * blocks + jj
             device = (block // n, block % n, lax.rem(c + k, parts))
             copy = remote(
@@ -358,8 +362,7 @@
     up_load.start()
 
     source = own_slot // blocks
-    from_self = c == source
-    for i in range(groups * n):
+    for i in [gg * n + lax.rem(m + d, n) for d in outward(n) for gg in range(groups)]:
         arrived = remote(
             disp.at[g, i], disp.at[g, i], disp_send_sem.at[0, 0], disp_recv_sem.at[i], peer
         )

time: 95.3 us -> 94.7 us (level)
  no operation moved by 1% of the time
where the time goes in v3:
time: 94.7 us; the launch traced here: 94.3 us
  Pallas kernels  93.4 us (99%)
    pallas_call x1, Pallas kernels, layer(): pl.pallas_call(functools.partial(layer_kernel, sizes), out_shape=(jax.Sha...  79.2 us
    pallas_call x1, Pallas kernels, attend_rows(): pl.pallas_call(attend_kernel, out_shape=jax.ShapeDtypeStruct(queries.shap...  12.2 us
    pallas_call x1, Pallas kernels, hand_over(): pl.pallas_call(hand_over_kernel, out_shape=tuple((jax.ShapeDtypeStruct(x....  2.04 us

profile of v3, /device:TPU:0, one launch (start us, length us, event | category | flops | bytes accessed | tf_op | source)
XLA Modules:
  0.0 94.3 jit_solution(17296412940260346088)
XLA Ops:
  0.6 12.2 %shard_map.122.att_hbm = bf16[24,4096]{1,0:T(8,128)(2,1)} custom-call(s32[24]{0:T(128)} %lengths.1, s32[24]{0:T(128)} %slots.1, bf16[24,4096]{1,0:T(8,128)(2,1)} %queries.1, bf16[24,512]{1,0:T(8,128)(2,1)} %new_keys.1, bf16[24,512]{1,0:T(8,128)(2,1)} %new_values.1, bf16[24,512,512]{2,1,0:T(8,128)(2,1)} %key_hbm.1, bf16[24,512,512]{2,1,0:T(8,128)(2,1)} %value_hbm.1), custom_call_target="tpu_custom_call" | custom-call | tf_op jit(solution)/shard_map/pallas_call | solution.py:184
  12.8 79.2 %shard_map.123 = (bf16[24,4096]{1,0:T(8,128)(2,1)}, bf16[8,24,1792]{2,1,0:T(8,128)(2,1)}) custom-call(bf16[24,4096]{1,0:T(8,128)(2,1)} %shard_map.122.att_hbm, bf16[24,4096]{1,0:T(8,128)(2,1)} %res_hbm.1, bf16[512,4096]{1,0:T(8,128)(2,1)} %w_hbm.1, bf16[4096,1792]{1,0:T(8,128)(2,1)} %gate_hbm.1, bf16[4096,1792]{1,0:T(8,128)(2,1)} %up_hbm.1), custom_call_target="tpu_custom_call" | custom-call | tf_op jit(solution)/shard_map/pallas_call | solution.py:710
  92.1 2.0 %shard_map.124 = (bf16[24,4096]{1,0:T(8,128)(2,1)}, bf16[8,24,1792]{2,1,0:T(8,128)(2,1)}) custom-call(bf16[24,4096]{1,0:T(8,128)(2,1)} %get-tuple-element.6.res_in, bf16[8,24,1792]{2,1,0:T(8,128)(2,1)} %get-tuple-element.7.act_in), custom_call_target="tpu_custom_call" | custom-call | tf_op jit(solution)/shard_map/pallas_call | solution.py:795
